TPU v7x, 32 devices: a whole 2x2x4 slice. The times are simulated.
32 devices in a mesh: gx: 4 (over y, x), gy: 2 (over core), gz: 4 (over z).
Axes of the slice: x: 2, y: 2, z: 4, core: 2. Of those that a mesh axis runs over, the one named last changes fastest.
Arguments:
- gradient: bfloat16 [32, 32, 16, 512], P(None, 'gx', 'gy', 'gz'), may hold values from -6 to 6
- noise_draw: bfloat16 [32, 32, 16, 512], P(None, 'gx', 'gy', 'gz'), may hold values from -6 to 6
- current: float32 [32, 32, 16, 512], P(None, 'gx', 'gy', 'gz'), may hold values from -6 to 6
- eigvectors: bfloat16 [32, 16, 512, 512], P('gx', 'gy', 'gz'), may hold values from -0.125 to 0.125
- eigvalues: float32 [512], replicated, may hold values from 0.05 to 50
- reaction: float32 [32, 16, 512], P('gx', 'gy', 'gz'), may hold values from 0.25 to 4
Outputs:
- proposal: float32 [32, 32, 16, 512], P(None, 'gx', 'gy', 'gz')
All inputs are finite; a program needn't handle non-finite values.
Results may differ from a plain program's by a relative error of at most 0.00031.
Values sent between devices are 32-bit elements; how exact they have to be, the bound alone decides.
A program may use at most 64 MiB of HBM per device.

v0:
```python
import jax
import jax.numpy as jnp
from jax import lax
from jax.sharding import PartitionSpec as P

SWEEPS = 4


def with_halo(block, sides, width):
    for axis, dim in sides:
        count = lax.axis_size(axis)
        forward = [(i, i + 1) for i in range(count - 1)]
        backward = [(target, source) for source, target in forward]
        low = lax.ppermute(
            lax.slice_in_dim(block, block.shape[dim] - width, None, axis=dim), axis, forward
        )
        high = lax.ppermute(lax.slice_in_dim(block, 0, width, axis=dim), axis, backward)
        block = jnp.concatenate([low, block, high], axis=dim)
    return block


def prior_root(source, reaction):
    sweeps = SWEEPS
    diagonal = reaction + 6.0
    field = source / diagonal
    for sweep_index in range(sweeps - 1):
        padded = with_halo(field, (("gx", 1), ("gy", 2), ("gz", 3)), 1)
        total = padded[:, 2:, 1:-1, 1:-1] + padded[:, :-2, 1:-1, 1:-1]
        total = total + padded[:, 1:-1, 2:, 1:-1] + padded[:, 1:-1, :-2, 1:-1]
        total = total + padded[:, 1:-1, 1:-1, 2:] + padded[:, 1:-1, 1:-1, :-2]
        field = (source + total) / diagonal
    return field


def body(gradient, noise_draw, current, eigvectors, eigvalues, reaction):
    chains = gradient.shape[0]
    rank = eigvectors.shape[3]
    cells = reaction.shape[0] * reaction.shape[1] * reaction.shape[2]
    basis = eigvectors.reshape(cells, rank)
    stacked = jnp.concatenate(
        [gradient.reshape(chains, cells), noise_draw.reshape(chains, cells)], 0
    )
    partial_sums = jnp.dot(stacked, basis, preferred_element_type=jnp.float32)
    local_part = -0.5 * gradient.astype(jnp.float32) + 1.0 * noise_draw.astype(jnp.float32)
    sums = lax.psum(partial_sums, ("gx", "gy", "gz"))
    damp = eigvalues / (eigvalues + 1.0)
    root_damp = 1.0 - 1.0 / jnp.sqrt(1.0 + eigvalues)
    coef = (0.5 * damp * sums[:chains] - 1.0 * root_damp * sums[chains:]).astype(jnp.bfloat16)
    corr = lax.dot_general(
        coef, basis, (((1,), (1,)), ((), ())), preferred_element_type=jnp.float32
    )
    field = prior_root(local_part + corr.reshape(current.shape), reaction)
    return current + field


def solution(mesh):
    return jax.shard_map(
        body,
        mesh=mesh,
        in_specs=(
            P(None, "gx", "gy", "gz"),
            P(None, "gx", "gy", "gz"),
            P(None, "gx", "gy", "gz"),
            P("gx", "gy", "gz", None),
            P(),
            P("gx", "gy", "gz"),
        ),
        out_specs=P(None, "gx", "gy", "gz"),
        check_vma=False,
    )
```

profile of v0, /device:TPU:0, one launch (start us, length us, event | category | flops | bytes accessed | tf_op | source)
XLA Modules:
  0.0 262.8 jit_solution(8625238853567087662)
XLA Ops:
  6.5 1.9 copy_bitcast_fusion
  8.4 5.7 %fusion.22 = f32[64,512]{1,0:T(8,128)} fusion(bf16[8192,512]{1,0:T(8,128)(2,1)} %bitcast.18, bf16[32,8192]{1,0:T(8,128)(2,1)S(1)} %get-tuple-element.27, bf16[32,8192]{1,0:T(8,128)(2,1)S(1)} %get-tuple-element.28), kind=kOutput, calls=%fused_computation.80 | convolution fusion | flops 538968064 | bytes 9568256 | tf_op jit(solution)/shard_map/dot_general | solution.py:43
  14.2 127.2 %all-reduce.2.cloned.1.call-done = f32[64,512]{1,0:T(8,128)} async-done(((f32[64,512]{1,0:T(8,128)}), f32[64,512]{1,0:T(8,128)}) %all-reduce.2.cloned.1.call-update) | async-done | bytes 131088 | tf_op jit(solution)/shard_map/psum | solution.py:45
  141.5 6.0 %broadcast_divide_fusion = (f32[32,8,8,128]{3,0,2,1:T(8,128)S(1)}, f32[32,8,8,128]{3,0,2,1:T(8,128)S(1)}) fusion(f32[8,8,128]{2,1,0:T(8,128)S(1)} %broadcast_add_fusion, bf16[8,8,128,512]{3,2,1,0:T(8,128)(2,1)} %param.9, f32[64,512]{1,0:T(8,128)} %all-reduce.2.cloned.1.call-done, f32[512]{0:T(512)S(1)} %get-tuple-element.24, f32[512]{0:T(512)S(1)} %get-tuple-element.23, ...), kind=kOutput, calls=%fused_computation.86 | convolution fusion | flops 270073856 | bytes 11702272 | tf_op jit(solution)/shard_map/dot_general | solution.py:49
  147.5 3.4 %collective-permute-start.1 = (f32[32,1,8,128]{3,0,2,1:T(8,128)S(1)}, f32[32,1,8,128]{3,0,2,1:T(8,128)S(1)}, u32[]{:S(2)}, u32[]{:S(2)}) collective-permute-start(f32[32,1,8,128]{3,0,2,1:T(8,128)S(1)} %get-tuple-element.21), channel_id=1, source_target_pairs={{0,8},{8,16},{16,24},{1,9},{9,17},{17,25},{2,10},{10,18},{18,26},{... | collective-permute-start | bytes 393224 | tf_op jit(solution)/shard_map/ppermute | solution.py:14
  153.4 4.7 %collective-permute-done = f32[32,1,8,128]{3,0,2,1:T(8,128)S(1)} collective-permute-done((f32[32,1,8,128]{3,0,2,1:T(8,128)S(1)}, f32[32,1,8,128]{3,0,2,1:T(8,128)S(1)}, u32[]{:S(2)}, u32[]{:S(2)}) %collective-permute-start) | collective-permute-done | bytes 131104 | tf_op jit(solution)/shard_map/ppermute | solution.py:17
  160.8 2.0 collective-permute-done.2
  163.4 2.3 fusion.37
  165.7 2.1 copy.13
  169.0 2.1 copy.15
  171.1 4.6 %collective-permute-start.5 = (f32[32,10,10,1]{0,3,2,1:T(1,128)S(1)}, f32[32,10,10,1]{0,3,2,1:T(1,128)S(1)}, u32[]{:S(2)}, u32[]{:S(2)}) collective-permute-start(f32[32,10,10,1]{0,3,2,1:T(1,128)S(1)} %copy.15), channel_id=1, source_target_pairs={{0,1},{1,2},{2,3},{4,5},{5,6},{6,7},{8,9},{9,10},{10,11},{12,13},{... | collective-permute-start | bytes 38408 | tf_op jit(solution)/shard_map/ppermute | solution.py:14
  177.5 1.9 copy.16
  179.4 2.9 %fusion.17 = f32[32,8,8,128]{3,0,2,1:T(8,128)S(1)} fusion(f32[32,8,8,128]{3,0,2,1:T(8,128)S(1)} %get-tuple-element.26, f32[32,10,10,1]{3,0,2,1:T(8,128)} %copy.16, f32[32,10,1,128]{3,0,2,1:T(8,128)} %copy-done.5, f32[32,10,1,128]{3,0,2,1:T(8,128)} %copy-done.3, f32[32,1,8,128]{3,0,2,1:T(8,128)S(1)} %collective-permute-done, ...), kind=kLoop, calls=%fused_computation.58 | loop fusion | flops 6553600 | bytes 3793920 | tf_op jit(solution)/shard_map/div | solution.py:31
  182.3 3.9 %collective-permute-start.7 = (f32[32,1,8,128]{3,0,2,1:T(8,128)S(1)}, f32[32,1,8,128]{3,0,2,1:T(8,128)S(1)}, u32[]{:S(2)}, u32[]{:S(2)}) collective-permute-start(f32[32,1,8,128]{3,0,2,1:T(8,128)S(1)} %get-tuple-element.19), channel_id=1, source_target_pairs={{0,8},{8,16},{16,24},{1,9},{9,17},{17,25},{2,10},{10,18},{18,26},{... | collective-permute-start | bytes 393224 | tf_op jit(solution)/shard_map/ppermute | solution.py:14
  188.8 4.4 %collective-permute-done.6 = f32[32,1,8,128]{3,0,2,1:T(8,128)S(1)} collective-permute-done((f32[32,1,8,128]{3,0,2,1:T(8,128)S(1)}, f32[32,1,8,128]{3,0,2,1:T(8,128)S(1)}, u32[]{:S(2)}, u32[]{:S(2)}) %collective-permute-start.6) | collective-permute-done | bytes 131104 | tf_op jit(solution)/shard_map/ppermute | solution.py:17
  195.8 2.0 collective-permute-done.8
  198.4 2.3 fusion.36
  200.7 2.1 copy.17
  204.0 2.1 copy.19
  206.1 4.8 %collective-permute-start.11 = (f32[32,10,10,1]{0,3,2,1:T(1,128)S(1)}, f32[32,10,10,1]{0,3,2,1:T(1,128)S(1)}, u32[]{:S(2)}, u32[]{:S(2)}) collective-permute-start(f32[32,10,10,1]{0,3,2,1:T(1,128)S(1)} %copy.19), channel_id=1, source_target_pairs={{0,1},{1,2},{2,3},{4,5},{5,6},{6,7},{8,9},{9,10},{10,11},{12,13},{... | collective-permute-start | bytes 38408 | tf_op jit(solution)/shard_map/ppermute | solution.py:14
  212.8 1.9 copy.20
  214.6 2.9 %fusion.10 = f32[32,8,8,128]{3,0,2,1:T(8,128)S(1)} fusion(f32[32,8,8,128]{3,0,2,1:T(8,128)S(1)} %get-tuple-element.26, f32[32,10,10,1]{3,0,2,1:T(8,128)} %copy.20, f32[32,10,1,128]{3,0,2,1:T(8,128)} %copy-done.6, f32[32,10,1,128]{3,0,2,1:T(8,128)} %copy-done.4, f32[32,1,8,128]{3,0,2,1:T(8,128)S(1)} %collective-permute-done.6, ...), kind=kLoop, calls=%fused_computation.33 | loop fusion | flops 6553600 | bytes 3793920 | tf_op jit(solution)/shard_map/div | solution.py:31
  217.5 3.4 %collective-permute-start.13 = (f32[32,1,8,128]{3,0,2,1:T(8,128)S(1)}, f32[32,1,8,128]{3,0,2,1:T(8,128)S(1)}, u32[]{:S(2)}, u32[]{:S(2)}) collective-permute-start(f32[32,1,8,128]{3,0,2,1:T(8,128)S(1)} %get-tuple-element.17), channel_id=1, source_target_pairs={{0,8},{8,16},{16,24},{1,9},{9,17},{17,25},{2,10},{10,18},{18,26},{... | collective-permute-start | bytes 393224 | tf_op jit(solution)/shard_map/ppermute | solution.py:14
  223.7 4.1 %collective-permute-done.12 = f32[32,1,8,128]{3,0,2,1:T(8,128)S(1)} collective-permute-done((f32[32,1,8,128]{3,0,2,1:T(8,128)S(1)}, f32[32,1,8,128]{3,0,2,1:T(8,128)S(1)}, u32[]{:S(2)}, u32[]{:S(2)}) %collective-permute-start.12) | collective-permute-done | bytes 131104 | tf_op jit(solution)/shard_map/ppermute | solution.py:17
  230.5 2.0 collective-permute-done.14
  233.1 2.2 fusion.35
  235.3 2.1 copy.21
  238.7 2.7 %copy.23 = f32[32,10,10,1]{0,3,2,1:T(1,128)} copy(f32[32,10,10,1]{3,0,2,1:T(8,128)} %get-tuple-element.6) | data formatting | bytes 25600 | tf_op jit(solution)/shard_map/slice | solution.py:15
  241.4 5.5 %collective-permute-start.17 = (f32[32,10,10,1]{0,3,2,1:T(1,128)}, f32[32,10,10,1]{0,3,2,1:T(1,128)}, u32[]{:S(2)}, u32[]{:S(2)}) collective-permute-start(f32[32,10,10,1]{0,3,2,1:T(1,128)} %copy.23), channel_id=1, source_target_pairs={{0,1},{1,2},{2,3},{4,5},{5,6},{6,7},{8,9},{9,10},{10,11},{12,13},{... | collective-permute-start | bytes 38408 | tf_op jit(solution)/shard_map/ppermute | solution.py:14
  246.9 1.9 copy.22
  248.8 2.6 %copy.24 = f32[32,10,10,1]{3,0,2,1:T(8,128)} copy(f32[32,10,10,1]{0,3,2,1:T(1,128)} %collective-permute-done.17) | data formatting | bytes 25600 | tf_op jit(solution)/shard_map/ppermute | solution.py:14
  251.4 3.0 %fusion.3 = f32[32,8,8,128]{3,0,2,1:T(8,128)S(1)} fusion(f32[32,8,8,128]{3,0,2,1:T(8,128)S(1)} %get-tuple-element.26, f32[32,10,10,1]{3,0,2,1:T(8,128)} %copy.24, f32[32,10,1,128]{3,0,2,1:T(8,128)} %copy-done.8, f32[32,10,1,128]{3,0,2,1:T(8,128)} %copy-done.7, f32[32,1,8,128]{3,0,2,1:T(8,128)S(1)} %collective-permute-done.12, ...), kind=kLoop, calls=%fused_computation.8 | loop fusion | flops 6815744 | bytes 4842496 | tf_op jit(solution)/shard_map/add | solution.py:53
  (62 shorter events, 26.8 us)
Async XLA Ops:
  6.5 134.9 %all-reduce.2.cloned.1.call-start = ((), (), s32[]{:S(2)}) async-start(), calls=%async_computation | async-start | bytes 262144 | tf_op jit(solution)/shard_map/psum | solution.py:45
  8.4 5.8 %copy-start.9 = (f32[8,8,128]{2,1,0:T(8,128)S(1)}, f32[8,8,128]{2,1,0:T(8,128)}, u32[]{:S(2)}) copy-start(f32[8,8,128]{2,1,0:T(8,128)} %param.11) | copy-start | bytes 98308
  8.4 5.8 %copy-start.10 = (f32[512]{0:T(512)S(1)}, f32[512]{0:T(512)}, u32[]{:S(2)}) copy-start(f32[512]{0:T(512)} %param.10) | copy-start | bytes 6148
  8.4 133.0 %copy-start = (bf16[32,8,8,128]{3,2,1,0:T(8,128)(2,1)S(1)}, bf16[32,8,8,128]{3,2,1,0:T(8,128)(2,1)}, u32[]{:S(2)}) copy-start(bf16[32,8,8,128]{3,2,1,0:T(8,128)(2,1)} %param.7) | copy-start | bytes 1572868
  8.4 133.0 %copy-start.1 = (bf16[32,8,8,128]{3,2,1,0:T(8,128)(2,1)S(1)}, bf16[32,8,8,128]{3,2,1,0:T(8,128)(2,1)}, u32[]{:S(2)}) copy-start(bf16[32,8,8,128]{3,2,1,0:T(8,128)(2,1)} %param.6) | copy-start | bytes 1572868
  147.5 5.9 %collective-permute-start.1 = (f32[32,1,8,128]{3,0,2,1:T(8,128)S(1)}, f32[32,1,8,128]{3,0,2,1:T(8,128)S(1)}, u32[]{:S(2)}, u32[]{:S(2)}) collective-permute-start(f32[32,1,8,128]{3,0,2,1:T(8,128)S(1)} %get-tuple-element.21), channel_id=1, source_target_pairs={{0,8},{8,16},{16,24},{1,9},{9,17},{17,25},{2,10},{10,18},{18,26},{... | collective-permute-start | bytes 393224 | tf_op jit(solution)/shard_map/ppermute | solution.py:14
  150.9 7.2 %collective-permute-start = (f32[32,1,8,128]{3,0,2,1:T(8,128)S(1)}, f32[32,1,8,128]{3,0,2,1:T(8,128)S(1)}, u32[]{:S(2)}, u32[]{:S(2)}) collective-permute-start(f32[32,1,8,128]{3,0,2,1:T(8,128)S(1)} %get-tuple-element.22), channel_id=1, source_target_pairs={{8,0},{16,8},{24,16},{9,1},{17,9},{25,17},{10,2},{18,10},{26,18},{... | collective-permute-start | bytes 393224 | tf_op jit(solution)/shard_map/ppermute | solution.py:17
  158.1 2.6 collective-permute-start.3
  159.5 3.3 %collective-permute-start.2 = (f32[32,10,1,128]{3,0,2,1:T(8,128)S(1)}, f32[32,10,1,128]{3,0,2,1:T(8,128)S(1)}, u32[]{:S(2)}, u32[]{:S(2)}) collective-permute-start(f32[32,10,1,128]{3,0,2,1:T(8,128)S(1)} %get-tuple-element.16), channel_id=1, source_target_pairs={{4,0},{5,1},{6,2},{7,3},{12,8},{13,9},{14,10},{15,11},{20,16},{21,... | collective-permute-start | bytes 491528 | tf_op jit(solution)/shard_map/ppermute | solution.py:17
  160.8 2.2 copy-start.3
  162.7 0.7 copy-start.5
  167.7 7.9 %collective-permute-start.4 = (f32[32,10,10,1]{0,3,2,1:T(1,128)S(1)}, f32[32,10,10,1]{0,3,2,1:T(1,128)S(1)}, u32[]{:S(2)}, u32[]{:S(2)}) collective-permute-start(f32[32,10,10,1]{0,3,2,1:T(1,128)S(1)} %copy.13), channel_id=1, source_target_pairs={{1,0},{2,1},{3,2},{5,4},{6,5},{7,6},{9,8},{10,9},{11,10},{13,12},{... | collective-permute-start | bytes 38408 | tf_op jit(solution)/shard_map/ppermute | solution.py:17
  171.1 6.4 %collective-permute-start.5 = (f32[32,10,10,1]{0,3,2,1:T(1,128)S(1)}, f32[32,10,10,1]{0,3,2,1:T(1,128)S(1)}, u32[]{:S(2)}, u32[]{:S(2)}) collective-permute-start(f32[32,10,10,1]{0,3,2,1:T(1,128)S(1)} %copy.15), channel_id=1, source_target_pairs={{0,1},{1,2},{2,3},{4,5},{5,6},{6,7},{8,9},{9,10},{10,11},{12,13},{... | collective-permute-start | bytes 38408 | tf_op jit(solution)/shard_map/ppermute | solution.py:14
  182.3 6.4 %collective-permute-start.7 = (f32[32,1,8,128]{3,0,2,1:T(8,128)S(1)}, f32[32,1,8,128]{3,0,2,1:T(8,128)S(1)}, u32[]{:S(2)}, u32[]{:S(2)}) collective-permute-start(f32[32,1,8,128]{3,0,2,1:T(8,128)S(1)} %get-tuple-element.19), channel_id=1, source_target_pairs={{0,8},{8,16},{16,24},{1,9},{9,17},{17,25},{2,10},{10,18},{18,26},{... | collective-permute-start | bytes 393224 | tf_op jit(solution)/shard_map/ppermute | solution.py:14
  186.3 6.9 %collective-permute-start.6 = (f32[32,1,8,128]{3,0,2,1:T(8,128)S(1)}, f32[32,1,8,128]{3,0,2,1:T(8,128)S(1)}, u32[]{:S(2)}, u32[]{:S(2)}) collective-permute-start(f32[32,1,8,128]{3,0,2,1:T(8,128)S(1)} %get-tuple-element.20), channel_id=1, source_target_pairs={{8,0},{16,8},{24,16},{9,1},{17,9},{25,17},{10,2},{18,10},{26,18},{... | collective-permute-start | bytes 393224 | tf_op jit(solution)/shard_map/ppermute | solution.py:17
  193.2 2.6 collective-permute-start.9
  194.5 3.3 %collective-permute-start.8 = (f32[32,10,1,128]{3,0,2,1:T(8,128)S(1)}, f32[32,10,1,128]{3,0,2,1:T(8,128)S(1)}, u32[]{:S(2)}, u32[]{:S(2)}) collective-permute-start(f32[32,10,1,128]{3,0,2,1:T(8,128)S(1)} %get-tuple-element.14), channel_id=1, source_target_pairs={{4,0},{5,1},{6,2},{7,3},{12,8},{13,9},{14,10},{15,11},{20,16},{21,... | collective-permute-start | bytes 491528 | tf_op jit(solution)/shard_map/ppermute | solution.py:17
  195.8 2.2 copy-start.4
  197.8 0.7 copy-start.6
  202.7 8.2 %collective-permute-start.10 = (f32[32,10,10,1]{0,3,2,1:T(1,128)S(1)}, f32[32,10,10,1]{0,3,2,1:T(1,128)S(1)}, u32[]{:S(2)}, u32[]{:S(2)}) collective-permute-start(f32[32,10,10,1]{0,3,2,1:T(1,128)S(1)} %copy.17), channel_id=1, source_target_pairs={{1,0},{2,1},{3,2},{5,4},{6,5},{7,6},{9,8},{10,9},{11,10},{13,12},{... | collective-permute-start | bytes 38408 | tf_op jit(solution)/shard_map/ppermute | solution.py:17
  206.1 6.6 %collective-permute-start.11 = (f32[32,10,10,1]{0,3,2,1:T(1,128)S(1)}, f32[32,10,10,1]{0,3,2,1:T(1,128)S(1)}, u32[]{:S(2)}, u32[]{:S(2)}) collective-permute-start(f32[32,10,10,1]{0,3,2,1:T(1,128)S(1)} %copy.19), channel_id=1, source_target_pairs={{0,1},{1,2},{2,3},{4,5},{5,6},{6,7},{8,9},{9,10},{10,11},{12,13},{... | collective-permute-start | bytes 38408 | tf_op jit(solution)/shard_map/ppermute | solution.py:14
  217.5 6.1 %collective-permute-start.13 = (f32[32,1,8,128]{3,0,2,1:T(8,128)S(1)}, f32[32,1,8,128]{3,0,2,1:T(8,128)S(1)}, u32[]{:S(2)}, u32[]{:S(2)}) collective-permute-start(f32[32,1,8,128]{3,0,2,1:T(8,128)S(1)} %get-tuple-element.17), channel_id=1, source_target_pairs={{0,8},{8,16},{16,24},{1,9},{9,17},{17,25},{2,10},{10,18},{18,26},{... | collective-permute-start | bytes 393224 | tf_op jit(solution)/shard_map/ppermute | solution.py:14
  220.9 6.9 %collective-permute-start.12 = (f32[32,1,8,128]{3,0,2,1:T(8,128)S(1)}, f32[32,1,8,128]{3,0,2,1:T(8,128)S(1)}, u32[]{:S(2)}, u32[]{:S(2)}) collective-permute-start(f32[32,1,8,128]{3,0,2,1:T(8,128)S(1)} %get-tuple-element.18), channel_id=1, source_target_pairs={{8,0},{16,8},{24,16},{9,1},{17,9},{25,17},{10,2},{18,10},{26,18},{... | collective-permute-start | bytes 393224 | tf_op jit(solution)/shard_map/ppermute | solution.py:17
  227.8 2.6 collective-permute-start.15
  229.1 3.3 %collective-permute-start.14 = (f32[32,10,1,128]{3,0,2,1:T(8,128)S(1)}, f32[32,10,1,128]{3,0,2,1:T(8,128)S(1)}, u32[]{:S(2)}, u32[]{:S(2)}) collective-permute-start(f32[32,10,1,128]{3,0,2,1:T(8,128)S(1)} %get-tuple-element.12), channel_id=1, source_target_pairs={{4,0},{5,1},{6,2},{7,3},{12,8},{13,9},{14,10},{15,11},{20,16},{21,... | collective-permute-start | bytes 491528 | tf_op jit(solution)/shard_map/ppermute | solution.py:17
  230.4 2.2 copy-start.7
  232.4 0.7 copy-start.8
  237.4 9.5 %collective-permute-start.16 = (f32[32,10,10,1]{0,3,2,1:T(1,128)S(1)}, f32[32,10,10,1]{0,3,2,1:T(1,128)S(1)}, u32[]{:S(2)}, u32[]{:S(2)}) collective-permute-start(f32[32,10,10,1]{0,3,2,1:T(1,128)S(1)} %copy.21), channel_id=1, source_target_pairs={{1,0},{2,1},{3,2},{5,4},{6,5},{7,6},{9,8},{10,9},{11,10},{13,12},{... | collective-permute-start | bytes 38408 | tf_op jit(solution)/shard_map/ppermute | solution.py:17
  241.4 10.0 %copy-start.2 = (f32[32,8,8,128]{3,2,1,0:T(8,128)S(1)}, f32[32,8,8,128]{3,2,1,0:T(8,128)}, u32[]{:S(2)}) copy-start(f32[32,8,8,128]{3,2,1,0:T(8,128)} %param.8) | copy-start | bytes 3145732
  241.4 7.4 %collective-permute-start.17 = (f32[32,10,10,1]{0,3,2,1:T(1,128)}, f32[32,10,10,1]{0,3,2,1:T(1,128)}, u32[]{:S(2)}, u32[]{:S(2)}) collective-permute-start(f32[32,10,10,1]{0,3,2,1:T(1,128)} %copy.23), channel_id=1, source_target_pairs={{0,1},{1,2},{2,3},{4,5},{5,6},{6,7},{8,9},{9,10},{10,11},{12,13},{... | collective-permute-start | bytes 38408 | tf_op jit(solution)/shard_map/ppermute | solution.py:14
Sparse Core Ops, SparseCore 0:
  14.3 127.1 all-reduce.1
where the time goes:
time: 264 us; the launch traced here: 263 us
  waiting for transfers between devices  150 us (57%)
  starting transfers between devices  41.1 us (16%)
  local copies, waits for them, and re-layouts  36.7 us (14%)
  between operations  13.8 us (5%)
  matrix products  11.7 us (4%)
  other arithmetic  9.37 us (4%)
    psum x1, waiting for transfers between devices, body(): sums = lax.psum(partial_sums, ('gx', 'gy', 'gz'))  127 us
    ppermute x9, starting transfers between devices, with_halo(): lax.ppermute(lax.slice_in_dim(block, block.shape[dim] - width, None, axis...  29.4 us
    ppermute x9, waiting for transfers between devices, with_halo(): lax.ppermute(lax.slice_in_dim(block, 0, width, axis=dim), axis, backward)  19.1 us
    slice x6, local copies, waits for them, and re-layouts, with_halo(): lax.slice_in_dim(block, 0, width, axis=dim)  13 us
    ppermute x9, starting transfers between devices, with_halo(): lax.ppermute(lax.slice_in_dim(block, 0, width, axis=dim), axis, backward)  11.6 us
    slice x6, local copies, waits for them, and re-layouts, with_halo(): lax.slice_in_dim(block, block.shape[dim] - width, None, axis=dim)  6.9 us
    ppermute x3, local copies, waits for them, and re-layouts, with_halo(): lax.ppermute(lax.slice_in_dim(block, block.shape[dim] - width, None, axis...  6.34 us
    dot_general x1, matrix products, body(): lax.dot_general(coef, basis, (((1,), (1,)), ((), ())), preferred_element_...  6.04 us
  transfers between devices with their start and end apart: 19, of which 10 were waited for; matrix products, arithmetic and copies ran while one was open for 5% of the time, Pallas kernels for 0%

commit v1 on v0

v1 whole, which is shorter than its diff:
```python
import functools

import jax
import jax.numpy as jnp
from jax import lax
from jax.experimental import pallas as pl
from jax.experimental.pallas import tpu as pltpu
from jax.sharding import PartitionSpec as P

SWEEPS = 4
GROUPS = 4
MESH = pl.DeviceIdType.MESH
AXES = ("gx", "gy", "gz")


def kernel(
    sizes, shape, g_h, n_h, cur_h, eig_h, ev_ref, rea_h, out_h,
    eig_v, gb, nb, gf, nf, cur_v, rdv, lhs, src, fields, zout, zin,
    part, got1, got2, full, load_sem, out_sem,
    send1, recv1, send2, recv2, send3, recv3, hsend, hrecv,
):
    C, X, Y, Z, R = shape
    NX, NY, NZ = sizes
    G = src.shape[0]
    CG = C // G
    XY = X * Y
    S = SWEEPS - 1
    PL = NX * NY
    rows = part.shape[1]
    pos = {a: lax.axis_index(a) for a in AXES}
    count = dict(zip(AXES, sizes))
    me_p = pos["gx"] * NY + pos["gy"]
    me_z = pos["gz"]

    loads = [
        pltpu.make_async_copy(g_h, gb, load_sem.at[0]),
        pltpu.make_async_copy(n_h, nb, load_sem.at[1]),
        pltpu.make_async_copy(rea_h, rdv, load_sem.at[2]),
        pltpu.make_async_copy(cur_h, cur_v, load_sem.at[3]),
    ]
    eig_loads = [
        pltpu.make_async_copy(eig_h.at[x], eig_v.at[x], load_sem.at[4 + x]) for x in range(X)
    ]
    for c in loads[:3] + eig_loads + loads[3:]:
        c.start()

    barrier = pltpu.get_barrier_semaphore()

    def plane_peer(d):
        q = lax.rem(me_p + d, PL)
        return {"gx": q // NY, "gy": lax.rem(q, NY)}, q

    for d in range(1, PL):
        pl.semaphore_signal(barrier, inc=1, device_id=plane_peer(d)[0], device_id_type=MESH)
    for d in range(1, NZ):
        pl.semaphore_signal(
            barrier, inc=1, device_id={"gz": lax.rem(me_z + d, NZ)}, device_id_type=MESH
        )

    zeros = jnp.zeros((Y, CG, Z), jnp.float32)
    zerosy = jnp.zeros((X, CG, Z), jnp.float32)

    def fill(cond, fn):
        if cond is True:
            fn()
        else:
            pl.when(cond)(fn)

    def low_edge(a):
        return True if count[a] == 1 else pos[a] == 0

    def high_edge(a):
        return True if count[a] == 1 else pos[a] == count[a] - 1

    for k in range(S):
        for g in range(G):
            def x0(k=k, g=g):
                fields[k, g, 0, 1 : Y + 1] = zeros
            def x1(k=k, g=g):
                fields[k, g, X + 1, 1 : Y + 1] = zeros
            def y0(k=k, g=g):
                fields[k, g, 1 : X + 1, 0] = zerosy
            def y1(k=k, g=g):
                fields[k, g, 1 : X + 1, Y + 1] = zerosy
            def z0(k=k, g=g):
                zin[k, g, 0] = jnp.zeros((CG, Z), jnp.float32)
            def z1(k=k, g=g):
                zin[k, g, 1] = jnp.zeros((CG, Z), jnp.float32)
            fill(low_edge("gx"), x0)
            fill(high_edge("gx"), x1)
            fill(low_edge("gy"), y0)
            fill(high_edge("gy"), y1)
            fill(low_edge("gz"), z0)
            fill(high_edge("gz"), z1)

    loads[0].wait()
    loads[1].wait()
    loads[2].wait()
    rdv[...] = 1.0 / (rdv[...] + 6.0)
    CH = XY
    @pl.loop(0, C)
    def _(c):
        r = pl.ds(pl.multiple_of(c * CH, CH), CH)
        gf[r, :] = gb[r, :].astype(jnp.float32)
        nf[r, :] = nb[r, :].astype(jnp.float32)

    @pl.loop(0, X)
    def _(x):
        for y in range(Y):
            at = pl.ds(x * Y + y, C, stride=XY)
            gv = gf[at, :]
            nv = nf[at, :]
            lhs[x, 0:C, y * Z : (y + 1) * Z] = gv.astype(jnp.bfloat16)
            lhs[x, C : 2 * C, y * Z : (y + 1) * Z] = nv.astype(jnp.bfloat16)
            s = -0.5 * gv + nv
            for g in range(G):
                src[g, x, y] = s[g * CG : (g + 1) * CG]

    acc = None
    for x in range(X):
        eig_loads[x].wait()
        term = jnp.dot(lhs[x], eig_v[x], preferred_element_type=jnp.float32)
        acc = term if acc is None else acc + term
    ev = ev_ref[...]
    damp = ev / (ev + 1.0)
    root_damp = 1.0 - 1.0 / jnp.sqrt(1.0 + ev)
    comb = (0.5 * damp) * acc[:C] - root_damp * acc[C:]
    RT = R // 128
    tiles = [(c, r) for c in range(C // 8) for r in range(RT)]
    for t, (c, r) in enumerate(tiles):
        tile = comb[c * 8 : (c + 1) * 8, r * 128 : (r + 1) * 128]
        if rows >= 8:
            o = (t * 8) % rows
            part[(t * 8) // rows, o : o + 8, :] = tile
        else:
            for j in range(8 // rows):
                part[(t * 8) // rows + j] = tile[j * rows : (j + 1) * rows]

    pl.semaphore_wait(barrier, PL - 1 + NZ - 1)

    copies1 = []
    for d in range(1, PL):
        dev, q = plane_peer(d)
        copies1.append(pltpu.make_async_remote_copy(
            src_ref=part.at[q], dst_ref=got1.at[d],
            send_sem=send1.at[d], recv_sem=recv1.at[d],
            device_id=dev, device_id_type=MESH))
    for c in copies1:
        c.start()
    total = part[me_p]
    for d in range(1, PL):
        copies1[d - 1].wait_recv()
        total = total + got1[d]
    got2[me_z] = total
    copies2 = []
    for d in range(1, NZ):
        copies2.append(pltpu.make_async_remote_copy(
            src_ref=got2.at[me_z], dst_ref=got2.at[me_z],
            send_sem=send2.at[d], recv_sem=recv2.at[d],
            device_id={"gz": lax.rem(me_z + d, NZ)}, device_id_type=MESH))
    for c in copies2:
        c.start()
    for c in copies2:
        c.wait_recv()
    total = got2[0]
    for j in range(1, NZ):
        total = total + got2[j]
    full[me_p] = total
    copies3 = []
    for d in range(1, PL):
        copies3.append(pltpu.make_async_remote_copy(
            src_ref=full.at[me_p], dst_ref=full.at[me_p],
            send_sem=send3.at[d], recv_sem=recv3.at[d],
            device_id=plane_peer(d)[0], device_id_type=MESH))
    for c in copies3:
        c.start()
    for c in copies3:
        c.wait_recv()
    bands = []
    for c in range(C // 8):
        band = []
        for r in range(RT):
            t = c * RT + r
            if rows >= 8:
                o = (t * 8) % rows
                band.append(full[(t * 8) // rows, o : o + 8, :])
            else:
                band.append(jnp.concatenate(
                    [full[(t * 8) // rows + j] for j in range(8 // rows)], 0))
        bands.append(jnp.concatenate(band, 1))
    coef = jnp.concatenate(bands, 0).astype(jnp.bfloat16)

    lane = lax.broadcasted_iota(jnp.int32, (CG, Z), 1)

    def halo(k, g, axis, sign):
        i = AXES.index(axis) * 2 + (sign > 0)
        if axis == "gx":
            s = fields.at[k, g, X if sign > 0 else 1, 1 : Y + 1]
            d = fields.at[k, g, 0 if sign > 0 else X + 1, 1 : Y + 1]
        elif axis == "gy":
            s = fields.at[k, g, 1 : X + 1, Y if sign > 0 else 1]
            d = fields.at[k, g, 1 : X + 1, 0 if sign > 0 else Y + 1]
        else:
            s = zout.at[k, g, 1 if sign > 0 else 0]
            d = zin.at[k, g, 0 if sign > 0 else 1]
        n = count[axis]
        to = lax.rem(pos[axis] + (sign + n), n)
        copy = pltpu.make_async_remote_copy(
            src_ref=s, dst_ref=d, send_sem=hsend.at[k, g, i], recv_sem=hrecv.at[k, g, i],
            device_id={axis: to}, device_id_type=MESH)
        up, down = pos[axis] < n - 1, pos[axis] > 0
        return copy, (up if sign > 0 else down), (down if sign > 0 else up)

    ways = [(a, s) for a in AXES if count[a] > 1 for s in (-1, 1)]

    def send(k, g, axes):
        for a, s in ways:
            if a in axes:
                copy, out, _ = halo(k, g, a, s)
                pl.when(out)(copy.start)

    def wait_halos(k, g):
        for a, s in ways:
            copy, _, come = halo(k, g, a, s)
            pl.when(come)(copy.wait_recv)

    def wait_sends(k, g):
        for a, s in ways:
            copy, out, _ = halo(k, g, a, s)
            pl.when(out)(copy.wait_send)

    def packed(x, y, f, low, high):
        l = x * Y + y
        low = jnp.where(lane == l, pltpu.roll(f, l, 1), low)
        high = jnp.where(lane == l, pltpu.roll(f, l + 1, 1), high)
        return low, high

    nothing = jnp.zeros((CG, Z), jnp.float32)

    def first(x, carry):
        corr = lax.dot_general(
            coef, eig_v[x], (((1,), (1,)), ((), ())), preferred_element_type=jnp.float32)
        rdx = rdv[x]
        carry = list(carry)
        for y in range(Y):
            for g in range(G):
                s = src[g, x, y] + corr[g * CG : (g + 1) * CG, y * Z : (y + 1) * Z]
                src[g, x, y] = s
                f = s * rdx[y : y + 1]
                fields[0, g, x + 1, y + 1] = f
                carry[2 * g], carry[2 * g + 1] = packed(x, y, f, carry[2 * g], carry[2 * g + 1])
        return tuple(carry)

    carry = first(0, (nothing,) * (2 * G))
    carry = first(X - 1, carry)
    for g in range(G):
        send(0, g, ("gx",))
    carry = lax.fori_loop(1, X - 1, first, carry)
    for g in range(G):
        zout[0, g, 0] = carry[2 * g]
        zout[0, g, 1] = carry[2 * g + 1]
    for g in range(G):
        send(0, g, ("gz", "gy"))

    loads[3].wait()
    outs = []
    for k in range(S):
        for g in range(G):
            wait_halos(k, g)
            zlo = zin[k, g, 0]
            zhi = zin[k, g, 1]

            def step(x, carry, k=k, g=g, zlo=zlo, zhi=zhi):
                rdx = rdv[x]
                low, high = carry
                for y in range(Y):
                    l = x * Y + y
                    f = fields[k, g, x + 1, y + 1]
                    t = fields[k, g, x + 2, y + 1] + fields[k, g, x, y + 1]
                    t = t + (fields[k, g, x + 1, y + 2] + fields[k, g, x + 1, y])
                    up = jnp.where(lane == Z - 1, pltpu.roll(zhi, Z - 1 - l, 1), pltpu.roll(f, Z - 1, 1))
                    down = jnp.where(lane == 0, pltpu.roll(zlo, lax.rem(Z - l, Z), 1), pltpu.roll(f, 1, 1))
                    v = (src[g, x, y] + (t + (up + down))) * rdx[y : y + 1]
                    if k < S - 1:
                        fields[k + 1, g, x + 1, y + 1] = v
                        low, high = packed(x, y, v, low, high)
                    else:
                        at = pl.ds(g * CG * XY + l, CG, stride=XY)
                        cur_v[at, :] = cur_v[at, :] + v
                return low, high

            low, high = lax.fori_loop(0, X, step, (nothing, nothing))
            if k < S - 1:
                zout[k + 1, g, 0] = low
                zout[k + 1, g, 1] = high
                send(k + 1, g, AXES)
            else:
                r = pl.ds(g * CG * XY, CG * XY)
                c = pltpu.make_async_copy(cur_v.at[r], out_h.at[r], out_sem.at[g])
                c.start()
                outs.append(c)
    for c in copies1 + copies2 + copies3:
        c.wait_send()
    for k in range(S):
        for g in range(G):
            wait_sends(k, g)
    for c in outs:
        c.wait()


def body(sizes, gradient, noise_draw, current, eigvectors, eigvalues, reaction):
    C, X, Y, Z = gradient.shape
    R = eigvectors.shape[3]
    NX, NY, NZ = sizes
    PL = NX * NY
    G = GROUPS
    CG = C // G
    S = SWEEPS - 1
    XY = X * Y
    f32, bf16 = jnp.float32, jnp.bfloat16
    rows = C * R // 128 // PL
    any_space = pl.BlockSpec(memory_space=pl.ANY)
    dma = pltpu.SemaphoreType.DMA
    out = pl.pallas_call(
        functools.partial(kernel, sizes, (C, X, Y, Z, R)),
        out_shape=jax.ShapeDtypeStruct((C * XY, Z), f32),
        in_specs=[any_space] * 4 + [pl.BlockSpec(memory_space=pltpu.VMEM), any_space],
        out_specs=any_space,
        scratch_shapes=[
            pltpu.VMEM((X, Y * Z, R), bf16),
            pltpu.VMEM((C * XY, Z), bf16),
            pltpu.VMEM((C * XY, Z), bf16),
            pltpu.VMEM((C * XY, Z), f32),
            pltpu.VMEM((C * XY, Z), f32),
            pltpu.VMEM((C * XY, Z), f32),
            pltpu.VMEM((X, Y, Z), f32),
            pltpu.VMEM((X, 2 * C, Y * Z), bf16),
            pltpu.VMEM((G, X, Y, CG, Z), f32),
            pltpu.VMEM((S, G, X + 2, Y + 2, CG, Z), f32),
            pltpu.VMEM((S, G, 2, CG, Z), f32),
            pltpu.VMEM((S, G, 2, CG, Z), f32),
            pltpu.VMEM((PL, rows, 128), f32),
            pltpu.VMEM((PL, rows, 128), f32),
            pltpu.VMEM((NZ, rows, 128), f32),
            pltpu.VMEM((PL, rows, 128), f32),
            dma((4 + X,)),
            dma((G,)),
            dma((PL,)), dma((PL,)),
            dma((NZ,)), dma((NZ,)),
            dma((PL,)), dma((PL,)),
            dma((S, G, 6)), dma((S, G, 6)),
        ],
        compiler_params=pltpu.CompilerParams(
            collective_id=0, has_side_effects=True, vmem_limit_bytes=48 * 1024 * 1024
        ),
    )(
        gradient.reshape(C * XY, Z),
        noise_draw.reshape(C * XY, Z),
        current.reshape(C * XY, Z),
        eigvectors.reshape(X, Y * Z, R),
        eigvalues.reshape(1, R),
        reaction,
    )
    return out.reshape(current.shape)


def solution(mesh):
    return jax.shard_map(
        functools.partial(body, tuple(mesh.shape[a] for a in AXES)),
        mesh=mesh,
        in_specs=(
            P(None, "gx", "gy", "gz"),
            P(None, "gx", "gy", "gz"),
            P(None, "gx", "gy", "gz"),
            P("gx", "gy", "gz", None),
            P(),
            P("gx", "gy", "gz"),
        ),
        out_specs=P(None, "gx", "gy", "gz"),
        check_vma=False,
    )
```

time: 264 us -> 46.9 us (0.18)
  waiting for transfers between devices: 150 us -> 0 us
  starting transfers between devices: 41.1 us -> 0 us
  Pallas kernels: 0 us -> 40.8 us
  local copies, waits for them, and re-layouts: 36.7 us -> 5.72 us
  between operations: 13.8 us -> 0.01 us
  matrix products: 11.7 us -> 0 us
  other arithmetic: 9.37 us -> 0 us
    psum x1 -> x0, waiting for transfers between devices: 127 us -> none  [body(): sums = lax.psum(partial_sums, ('gx', 'gy', 'gz'))]
    ppermute x18 -> x0, starting transfers between devices: 41.1 us -> none  [the longest x9 29.4 us: with_halo(): lax.ppermute(lax.slice_in_dim(block, block.shape[dim] - width, None, axis...]
    pallas_call x0 -> x1, Pallas kernels: none -> 40.8 us  [body(): pl.pallas_call(functools.partial(kernel, sizes, (C, X, Y, Z, R)), out_sha...]
    ppermute x18 -> x0, waiting for transfers between devices: 23 us -> none  [the longest x9 19.1 us: with_halo(): lax.ppermute(lax.slice_in_dim(block, 0, width, axis=dim), axis, backward)]
    slice x12 -> x0, local copies, waits for them, and re-layouts: 19.9 us -> none  [the longest x6 13 us: with_halo(): lax.slice_in_dim(block, 0, width, axis=dim)]
    ppermute x6 -> x0, local copies, waits for them, and re-layouts: 11.9 us -> none  [the longest x3 6.34 us: with_halo(): lax.ppermute(lax.slice_in_dim(block, block.shape[dim] - width, None, axis...]
    dot_general x2 -> x0, matrix products: 11.7 us -> none  [the longest x1 6.04 us: body(): lax.dot_general(coef, basis, (((1,), (1,)), ((), ())), preferred_element_...]
    div x2 -> x0, other arithmetic: 5.8 us -> none  [prior_root(): field = (source + total) / diagonal]
  transfers between devices with their start and end apart: 19 -> 0, of which waited for: 10 -> 0; matrix products, arithmetic and copies ran while one was open for 5% -> 0% of each run, Pallas kernels for 0% -> 0%
where the time goes in v1:
time: 46.9 us; the launch traced here: 46.5 us
  Pallas kernels  40.8 us (87%)
  local copies, waits for them, and re-layouts  5.72 us (12%)
    pallas_call x1, Pallas kernels, body(): pl.pallas_call(functools.partial(kernel, sizes, (C, X, Y, Z, R)), out_sha...  40.8 us
    unnamed x11, local copies, waits for them, and re-layouts  5.72 us

profile of v1, /device:TPU:0, one launch (start us, length us, event | category | flops | bytes accessed | tf_op | source)
XLA Modules:
  0.0 46.5 jit_solution(12561581584546474104)
XLA Ops:
  0.0 0.0 copy-start
  0.0 1.2 %copy-done = f32[32,8,8,128]{3,2,1,0:T(8,128)S(1)} copy-done((f32[32,8,8,128]{3,2,1,0:T(8,128)S(1)}, f32[32,8,8,128]{3,2,1,0:T(8,128)}, u32[]{:S(2)}) %copy-start) | copy-done | bytes 1048600
  1.2 0.0 copy-start.1
  1.2 1.0 %copy-done.1 = bf16[32,8,8,128]{3,2,1,0:T(8,128)(2,1)S(1)} copy-done((bf16[32,8,8,128]{3,2,1,0:T(8,128)(2,1)S(1)}, bf16[32,8,8,128]{3,2,1,0:T(8,128)(2,1)}, u32[]{:S(2)}) %copy-start.1) | copy-done | bytes 524312
  2.3 0.0 copy-start.2
  2.3 1.0 %copy-done.2 = bf16[32,8,8,128]{3,2,1,0:T(8,128)(2,1)S(1)} copy-done((bf16[32,8,8,128]{3,2,1,0:T(8,128)(2,1)S(1)}, bf16[32,8,8,128]{3,2,1,0:T(8,128)(2,1)}, u32[]{:S(2)}) %copy-start.2) | copy-done | bytes 524312
  3.3 0.0 copy-start.3
  3.3 0.8 %copy-done.3 = f32[8,8,128]{2,1,0:T(8,128)S(1)} copy-done((f32[8,8,128]{2,1,0:T(8,128)S(1)}, f32[8,8,128]{2,1,0:T(8,128)}, u32[]{:S(2)}) %copy-start.3) | copy-done | bytes 32792
  4.1 0.0 copy-start.4
  4.1 0.7 %copy-done.4 = f32[512]{0:T(512)S(1)} copy-done((f32[512]{0:T(512)S(1)}, f32[512]{0:T(512)}, u32[]{:S(2)}) %copy-start.4) | copy-done | bytes 2072
  4.8 40.8 %shard_map.64 = f32[2048,128]{1,0:T(8,128)S(1)} custom-call(bf16[2048,128]{1,0:T(8,128)(2,1)S(1)} %bitcast.8, bf16[2048,128]{1,0:T(8,128)(2,1)S(1)} %bitcast.9, f32[2048,128]{1,0:T(8,128)S(1)} %bitcast.7, bf16[8,1024,512]{2,1,0:T(8,128)(2,1)} %bitcast.11, f32[1,512]{1,0:T(1,128)S(1)} %bitcast.10, f32[8,8,128]{2,1,0:T(8,128)S(1)} %copy-done.3), custom_call_target="tpu_custom_call" | custom-call | tf_op jit(solution)/shard_map/pallas_call | solution.py:324
  45.6 1.0 %copy.8 = f32[32,8,8,128]{3,2,1,0:T(8,128)} copy(f32[32,8,8,128]{3,2,1,0:T(8,128)S(1)} %bitcast.6) | data formatting | bytes 2097152
Async XLA Ops:
  0.0 1.2 %copy-start = (f32[32,8,8,128]{3,2,1,0:T(8,128)S(1)}, f32[32,8,8,128]{3,2,1,0:T(8,128)}, u32[]{:S(2)}) copy-start(f32[32,8,8,128]{3,2,1,0:T(8,128)} %param.8) | copy-start | bytes 3145732
  1.2 1.0 %copy-start.1 = (bf16[32,8,8,128]{3,2,1,0:T(8,128)(2,1)S(1)}, bf16[32,8,8,128]{3,2,1,0:T(8,128)(2,1)}, u32[]{:S(2)}) copy-start(bf16[32,8,8,128]{3,2,1,0:T(8,128)(2,1)} %param.6) | copy-start | bytes 1572868
  2.3 1.0 %copy-start.2 = (bf16[32,8,8,128]{3,2,1,0:T(8,128)(2,1)S(1)}, bf16[32,8,8,128]{3,2,1,0:T(8,128)(2,1)}, u32[]{:S(2)}) copy-start(bf16[32,8,8,128]{3,2,1,0:T(8,128)(2,1)} %param.7) | copy-start | bytes 1572868
  3.3 0.8 %copy-start.3 = (f32[8,8,128]{2,1,0:T(8,128)S(1)}, f32[8,8,128]{2,1,0:T(8,128)}, u32[]{:S(2)}) copy-start(f32[8,8,128]{2,1,0:T(8,128)} %rea_h.1) | copy-start | bytes 98308
  4.1 0.7 %copy-start.4 = (f32[512]{0:T(512)S(1)}, f32[512]{0:T(512)}, u32[]{:S(2)}) copy-start(f32[512]{0:T(512)} %param.10) | copy-start | bytes 6148

commit v2 on v1

--- a/solution.py
+++ b/solution.py
@@ -8,7 +8,7 @@
 from jax.sharding import PartitionSpec as P
 
 SWEEPS = 4
-GROUPS = 4
+GROUPS = 2
 MESH = pl.DeviceIdType.MESH
 AXES = ("gx", "gy", "gz")
 
@@ -270,26 +270,34 @@
             zlo = zin[k, g, 0]
             zhi = zin[k, g, 1]
 
-            def step(x, carry, k=k, g=g, zlo=zlo, zhi=zhi):
+            def step(x, carry, k=k, g=g):
                 rdx = rdv[x]
-                low, high = carry
+                low, high, zlo, zhi = carry
+                low = pltpu.roll(low, Z - Y, 1)
+                high = pltpu.roll(high, Z - Y, 1)
+                done = []
                 for y in range(Y):
-                    l = x * Y + y
                     f = fields[k, g, x + 1, y + 1]
                     t = fields[k, g, x + 2, y + 1] + fields[k, g, x, y + 1]
                     t = t + (fields[k, g, x + 1, y + 2] + fields[k, g, x + 1, y])
-                    up = jnp.where(lane == Z - 1, pltpu.roll(zhi, Z - 1 - l, 1), pltpu.roll(f, Z - 1, 1))
-                    down = jnp.where(lane == 0, pltpu.roll(zlo, lax.rem(Z - l, Z), 1), pltpu.roll(f, 1, 1))
+                    up = jnp.where(lane == Z - 1, pltpu.roll(zhi, Z - 1 - y, 1), pltpu.roll(f, Z - 1, 1))
+                    down = jnp.where(lane == 0, pltpu.roll(zlo, (Z - y) % Z, 1), pltpu.roll(f, 1, 1))
                     v = (src[g, x, y] + (t + (up + down))) * rdx[y : y + 1]
                     if k < S - 1:
+                        m = (X - 1) * Y + y
+                        low = jnp.where(lane == m, pltpu.roll(v, m, 1), low)
+                        high = jnp.where(lane == m, pltpu.roll(v, m + 1, 1), high)
+                    else:
+                        v = v + cur_v[pl.ds(g * CG * XY + x * Y + y, CG, stride=XY), :]
+                    done.append(v)
+                for y, v in enumerate(done):
+                    if k < S - 1:
                         fields[k + 1, g, x + 1, y + 1] = v
-                        low, high = packed(x, y, v, low, high)
                     else:
-                        at = pl.ds(g * CG * XY + l, CG, stride=XY)
-                        cur_v[at, :] = cur_v[at, :] + v
-                return low, high
-
-            low, high = lax.fori_loop(0, X, step, (nothing, nothing))
+                        cur_v[pl.ds(g * CG * XY + x * Y + y, CG, stride=XY), :] = v
+                return low, high, pltpu.roll(zlo, Z - Y, 1), pltpu.roll(zhi, Z - Y, 1)
+
+            low, high, _, _ = lax.fori_loop(0, X, step, (nothing, nothing, zlo, zhi))
             if k < S - 1:
                 zout[k + 1, g, 0] = low
                 zout[k + 1, g, 1] = high
@@ -351,7 +359,7 @@
             dma((S, G, 6)), dma((S, G, 6)),
         ],
         compiler_params=pltpu.CompilerParams(
-            collective_id=0, has_side_effects=True, vmem_limit_bytes=48 * 1024 * 1024
+            collective_id=0, has_side_effects=True, vmem_limit_bytes=67043328
         ),
     )(
         gradient.reshape(C * XY, Z),

time: 46.9 us -> 44.9 us (0.957)
  local copies, waits for them, and re-layouts: 5.72 us -> 2.31 us
  Pallas kernels: 40.8 us -> 42.4 us
    unnamed x11 -> x1, local copies, waits for them, and re-layouts: 5.72 us -> 2.31 us
    pallas_call x1, Pallas kernels: 40.8 us -> 42.4 us  [body(): pl.pallas_call(functools.partial(kernel, sizes, (C, X, Y, Z, R)), out_sha...]
where the time goes in v2:
time: 44.9 us; the launch traced here: 44.7 us
  Pallas kernels  42.4 us (94%)
  local copies, waits for them, and re-layouts  2.31 us (5%)
    pallas_call x1, Pallas kernels, body(): pl.pallas_call(functools.partial(kernel, sizes, (C, X, Y, Z, R)), out_sha...  42.4 us
    unnamed x1, local copies, waits for them, and re-layouts  2.31 us

profile of v2, /device:TPU:0, one launch (start us, length us, event | category | flops | bytes accessed | tf_op | source)
XLA Modules:
  0.0 44.7 jit_solution(9632977238318096339)
XLA Ops:
  0.0 42.4 %shard_map.64 = f32[2048,128]{1,0:T(8,128)} custom-call(bf16[2048,128]{1,0:T(8,128)(2,1)} %bitcast.9, bf16[2048,128]{1,0:T(8,128)(2,1)} %bitcast.10, f32[2048,128]{1,0:T(8,128)} %bitcast.8, bf16[8,1024,512]{2,1,0:T(8,128)(2,1)} %bitcast.6, f32[1,512]{1,0:T(1,128)} %bitcast.11, f32[8,8,128]{2,1,0:T(8,128)} %rea_h.1), custom_call_target="tpu_custom_call" | custom-call | tf_op jit(solution)/shard_map/pallas_call | solution.py:332
  42.4 2.3 %copy.8 = f32[32,8,8,128]{3,2,1,0:T(8,128)} copy(f32[32,8,8,128]{3,2,1,0:T(8,128)} %bitcast.7) | data formatting | bytes 2097152
